TPU v7x, 32 devices: a whole 2x2x4 slice. The times are simulated.
32 devices in a mesh: groups: 2 (over x), blk: 16 (over z, y, core).
Axes of the slice: x: 2, y: 2, z: 4, core: 2. Of those that a mesh axis runs over, the one named last changes fastest.
Arguments:
- queries: bfloat16 [4096, 4096], P(('groups', 'blk')), parts along dimension 0, may hold values from -96 to 96
- keys: bfloat16 [4096, 512], P(('groups', 'blk')), parts along dimension 0, may hold values from -3 to 3
- values: bfloat16 [4096, 512], P(('groups', 'blk')), parts along dimension 0, may hold values from -4 to 4
- out_packed: int32 [4096, 512], P('blk'), may hold values from -2147483648 to 2147483646
- out_scales: bfloat16 [32, 4096], replicated, may hold values from 0.0029907227 to 0.029907227
- hadamard_signs: int32 [4096], replicated, may hold values from 0 to 1
Outputs:
- mixed: bfloat16 [4096, 4096], P(('groups', 'blk')), parts along dimension 0
There are 2 independent parts, one for each index of `groups`. A program takes and returns all parts, laid end to end along the dimension named above; an argument that names none is the same for every part. Nothing has to cross between parts.
All inputs are finite; a program needn't handle non-finite values.
Results may differ from a plain program's by a relative error of at most 0.012.
Values may be sent and summed in bfloat16 or wider, within the bound.
A program may use at most 256 MiB of HBM per device.

v0:
```python
import math
import jax
import jax.numpy as jnp
from jax import lax
from jax.sharding import PartitionSpec as P

HEAD_SIZE = 128
QUERY_HEADS = 32
KEY_VALUE_HEADS = 4
GROUP = 128
masked_fill_value = -1e30


def sylvester(block_count):
    index = jnp.arange(block_count, dtype=jnp.int32)
    both = jnp.bitwise_and(index[:, None], index[None, :])
    parity = jnp.zeros((block_count, block_count), jnp.int32)
    for bit_number in range(block_count.bit_length() - 1):
        parity = jnp.bitwise_xor(parity, jnp.bitwise_and(jnp.right_shift(both, bit_number), 1))
    return (1 - 2 * parity).astype(jnp.bfloat16)


def rotate(attention, hadamard_signs):
    block_count = attention.shape[0]
    signed = (attention * (2 * hadamard_signs - 1).astype(jnp.bfloat16)).reshape(
        block_count, QUERY_HEADS, HEAD_SIZE
    )
    outer = jnp.einsum(
        "gh,rhd->rgd", sylvester(QUERY_HEADS), signed, preferred_element_type=jnp.float32
    )
    upper = outer.astype(jnp.bfloat16)
    lower = (outer - upper.astype(jnp.float32)).astype(jnp.bfloat16)
    inner_table = sylvester(HEAD_SIZE)
    inner = jnp.einsum("rgd,de->rge", upper, inner_table, preferred_element_type=jnp.float32)
    inner = inner + jnp.einsum(
        "rgd,de->rge", lower, inner_table, preferred_element_type=jnp.float32
    )
    return (
        (inner * (1.0 / math.sqrt(QUERY_HEADS * HEAD_SIZE)))
        .reshape(block_count, QUERY_HEADS * HEAD_SIZE)
        .astype(jnp.bfloat16)
    )


def dequantize_rows(packed, out_scales):
    block_count = packed.shape[0]
    group_count = out_scales.shape[0]
    group_index = jnp.arange(block_count, dtype=jnp.int32) // GROUP
    member = (group_index[:, None] == jnp.arange(group_count, dtype=jnp.int32)[None, :]).astype(
        jnp.bfloat16
    )
    scale_rows = jnp.dot(member, out_scales, preferred_element_type=jnp.float32)
    fields = [jnp.bitwise_and(jnp.right_shift(packed, 4 * nibble), 15) for nibble in range(8)]
    levels = jnp.concatenate(fields, axis=1) - 8
    return (levels.astype(jnp.float32) * scale_rows).astype(jnp.bfloat16)


def update(state, query_tile, query_positions, key_block, value_block, key_positions):
    largest, totals, summed = state
    scores = jnp.einsum("qkgd,nkd->kgqn", query_tile, key_block, preferred_element_type=jnp.float32)
    scores = scores * (1.0 / math.sqrt(HEAD_SIZE))
    allowed = query_positions[:, None] >= key_positions[None, :]
    scores = jnp.where(allowed, scores, masked_fill_value)
    new_largest = jnp.maximum(largest, jnp.max(scores, axis=-1))
    fading = jnp.exp(largest - new_largest)
    weights = jnp.exp(scores - new_largest[..., None])
    totals = totals * fading + jnp.sum(weights, axis=-1)
    product = jnp.einsum(
        "kgqn,nkd->qkgd",
        weights.astype(jnp.bfloat16),
        value_block,
        preferred_element_type=jnp.float32,
    )
    summed = summed * jnp.transpose(fading, (2, 0, 1))[..., None] + product
    return (new_largest, totals, summed)


def keep_state(current):
    return current


def local(queries, keys, values, out_packed, out_scales, hadamard_signs):
    sequence_rows = queries.shape[0]
    my_index = lax.axis_index("blk")
    head_group = QUERY_HEADS // KEY_VALUE_HEADS
    query_positions = my_index * sequence_rows + jnp.arange(sequence_rows, dtype=jnp.int32)
    rows_of_queries = queries.reshape(sequence_rows, KEY_VALUE_HEADS, head_group, HEAD_SIZE)
    initial = (
        jnp.full((KEY_VALUE_HEADS, head_group, sequence_rows), masked_fill_value, jnp.float32),
        jnp.zeros((KEY_VALUE_HEADS, head_group, sequence_rows), jnp.float32),
        jnp.zeros((sequence_rows, KEY_VALUE_HEADS, head_group, HEAD_SIZE), jnp.float32),
    )
    last_position = jnp.max(query_positions)
    key_slice = lax.all_gather(keys, "blk", axis=0, tiled=True)
    value_slice = lax.all_gather(values, "blk", axis=0, tiled=True)
    block_count = key_slice.shape[0]
    width = math.gcd(block_count, 512)
    heads_of_keys = key_slice.reshape(block_count, KEY_VALUE_HEADS, HEAD_SIZE)
    heads_of_values = value_slice.reshape(block_count, KEY_VALUE_HEADS, HEAD_SIZE)

    def sweep(current):

        def one_step(turn, inner_state):
            begin = turn * width
            key_block = lax.dynamic_slice_in_dim(heads_of_keys, begin, width, 0)
            value_block = lax.dynamic_slice_in_dim(heads_of_values, begin, width, 0)
            key_positions = begin + jnp.arange(width, dtype=jnp.int32)
            return update(
                inner_state, rows_of_queries, query_positions, key_block, value_block, key_positions
            )

        return lax.fori_loop(0, block_count // width, one_step, current)

    final = lax.cond(jnp.int32(0) <= last_position, sweep, keep_state, initial)
    largest, totals, summed = final
    attention = (
        (summed / jnp.transpose(totals, (2, 0, 1))[..., None])
        .reshape(sequence_rows, QUERY_HEADS * HEAD_SIZE)
        .astype(jnp.bfloat16)
    )
    rotated = rotate(attention, hadamard_signs)
    weight = dequantize_rows(lax.all_gather(out_packed, "blk", axis=0, tiled=True), out_scales)
    mixed = jnp.dot(rotated, weight, preferred_element_type=jnp.float32)
    return mixed.astype(jnp.bfloat16)


def solution(mesh):
    in_specs = (
        P(("groups", "blk"), None),
        P(("groups", "blk"), None),
        P(("groups", "blk"), None),
        P("blk", None),
        P(),
        P(),
    )
    out_specs = P(("groups", "blk"), None)
    return jax.shard_map(local, mesh=mesh, in_specs=in_specs, out_specs=out_specs, check_vma=False)
```

profile of v0, /device:TPU:0, one launch (start us, length us, event | category | flops | bytes accessed | tf_op | source)
XLA Modules:
  0.0 240.5 jit_solution(12664698832807533376)
XLA Ops:
  6.5 1.7 copy.25
  8.3 0.0 all-gather.6.cloned.1.call-start
  8.3 1.7 copy.26
  10.0 0.0 all-gather.8.cloned.1.call-start
  10.0 0.7 all-gather.8.cloned.1.call-update
  10.7 0.6 fusion.73
  11.9 0.7 fusion.47
  12.6 40.6 %all-gather.4.cloned.1.call-done = bf16[2048,512]{0,1:T(8,128)(2,1)} async-done(((bf16[128,512]{0,1:T(8,128)(2,1)}), bf16[2048,512]{0,1:T(8,128)(2,1)}) %all-gather.4.cloned.1.call-update) | async-done | bytes 2097168 | tf_op jit(solution)/shard_map/all_gather | solution.py:94
  53.3 42.3 %all-gather.6.cloned.1.call-done = bf16[2048,512]{0,1:T(8,128)(2,1)} async-done(((bf16[128,512]{0,1:T(8,128)(2,1)}), bf16[2048,512]{0,1:T(8,128)(2,1)}) %all-gather.6.cloned.1.call-update) | async-done | bytes 2097168 | tf_op jit(solution)/shard_map/all_gather | solution.py:95
  95.6 69.5 %conditional.1 = (f32[4,8,128]{2,1,0:T(8,128)}, f32[128,4,8,128]{0,3,2,1:T(8,128)}) conditional(s32[]{:T(128)} %convert_element_type.53, () %tuple.27, (bf16[2048,512]{0,1:T(8,128)(2,1)}, bf16[2048,512]{0,1:T(8,128)(2,1)}, bf16[128,4096]{1,0:T(8,128)(2,1)}, s32[128]{0:T(128)S(1)}) %tuple.28), branch_computations={%region_1.0_spmd, %region_2.7_spmd} | conditional | flops 1098473984 | bytes 69735248 | solution.py:114
  95.6 1.6 copy.27
  97.2 0.7 copy.24
  97.9 67.2 %while.17 = (s32[]{:T(128)}, f32[4,8,128]{2,1,0:T(8,128)S(1)}, f32[4,8,128]{2,1,0:T(8,128)}, f32[128,4,8,128]{0,3,2,1:T(8,128)}, s32[128]{0:T(128)S(1)}, /*index...) while((s32[]{:T(128)}, f32[4,8,128]{2,1,0:T(8,128)S(1)}, ...), condition=%wide.region_6.6_spmd.clone, body=%wide.region_3.5_spmd.clone.sunk | while | flops 1098473984 | bytes 65540820 | solution.py:112
  97.9 0.1 broadcast_compare_fusion.2
  98.1 5.7 %fusion.87 = (f32[4,8,128]{2,1,0:T(8,128)S(1)}, f32[4,512,128,8]{2,1,3,0:T(8,128)}) fusion(pred[128,512]{0,1:T(8,128)(4,1)S(1)} %broadcast_compare_fusion.2, bf16[128,4,8,128]{3,0,2,1:T(8,128)(2,1)S(1)} %get-tuple-element.326, bf16[2048,4,128]{0,2,1:T(8,128)(2,1)} %get-tuple-element.325, s32[]{:T(128)S(6)} %select_n.46), kind=kOutput, calls=%fused_computation.4.clone.1 | convolution fusion | flops 543158272 | bytes 10043396 | tf_op jit(solution)/shard_map/cond/branch_1_fun/while/body/eval_jaxpr/qkgd,nkd->kgqn/dot_general | solution.py:60
  103.8 7.6 %bitcast_add_fusion.2 = f32[128,4,8,128]{0,3,2,1:T(8,128)} fusion(f32[128,4,8,128]{0,3,2,1:T(8,128)} %get-tuple-element.311, f32[4,512,128,8]{2,1,3,0:T(8,128)} %get-tuple-element.294, f32[4,8,128]{2,1,0:T(8,128)S(1)} %get-tuple-element.321, pred[128,512]{0,1:T(8,128)(4,1)S(1)} %broadcast_compare_fusion.2, f32[128,4,8]{0,2,1:T(8,128)S(1)} %get-tuple-element.295, ...), kind=kOutput, calls=%fused_computation.10.clone.1 | convolution fusion | flops 546832384 | bytes 13205509 | tf_op jit(solution)/shard_map/cond/branch_1_fun/while/body/eval_jaxpr/kgqn,nkd->qkgd/dot_general | solution.py:68
  111.4 1.8 fusion.89
  113.2 0.6 fusion.90
  113.9 0.1 broadcast_compare_fusion.2
  114.0 5.7 %fusion.87 = (f32[4,8,128]{2,1,0:T(8,128)S(1)}, f32[4,512,128,8]{2,1,3,0:T(8,128)}) fusion(pred[128,512]{0,1:T(8,128)(4,1)S(1)} %broadcast_compare_fusion.2, bf16[128,4,8,128]{3,0,2,1:T(8,128)(2,1)S(1)} %get-tuple-element.326, bf16[2048,4,128]{0,2,1:T(8,128)(2,1)} %get-tuple-element.325, s32[]{:T(128)S(6)} %select_n.46), kind=kOutput, calls=%fused_computation.4.clone.1 | convolution fusion | flops 543158272 | bytes 10043396 | tf_op jit(solution)/shard_map/cond/branch_1_fun/while/body/eval_jaxpr/qkgd,nkd->kgqn/dot_general | solution.py:60
  119.8 7.9 %bitcast_add_fusion.2 = f32[128,4,8,128]{0,3,2,1:T(8,128)} fusion(f32[128,4,8,128]{0,3,2,1:T(8,128)} %get-tuple-element.311, f32[4,512,128,8]{2,1,3,0:T(8,128)} %get-tuple-element.294, f32[4,8,128]{2,1,0:T(8,128)S(1)} %get-tuple-element.321, pred[128,512]{0,1:T(8,128)(4,1)S(1)} %broadcast_compare_fusion.2, f32[128,4,8]{0,2,1:T(8,128)S(1)} %get-tuple-element.295, ...), kind=kOutput, calls=%fused_computation.10.clone.1 | convolution fusion | flops 546832384 | bytes 13205509 | tf_op jit(solution)/shard_map/cond/branch_1_fun/while/body/eval_jaxpr/kgqn,nkd->qkgd/dot_general | solution.py:68
  127.6 1.8 fusion.89
  129.4 1.3 fusion.90
  130.8 0.1 broadcast_compare_fusion.2
  130.9 5.8 %fusion.87 = (f32[4,8,128]{2,1,0:T(8,128)S(1)}, f32[4,512,128,8]{2,1,3,0:T(8,128)}) fusion(pred[128,512]{0,1:T(8,128)(4,1)S(1)} %broadcast_compare_fusion.2, bf16[128,4,8,128]{3,0,2,1:T(8,128)(2,1)S(1)} %get-tuple-element.326, bf16[2048,4,128]{0,2,1:T(8,128)(2,1)} %get-tuple-element.325, s32[]{:T(128)S(6)} %select_n.46), kind=kOutput, calls=%fused_computation.4.clone.1 | convolution fusion | flops 543158272 | bytes 10043396 | tf_op jit(solution)/shard_map/cond/branch_1_fun/while/body/eval_jaxpr/qkgd,nkd->kgqn/dot_general | solution.py:60
  136.7 8.0 %bitcast_add_fusion.2 = f32[128,4,8,128]{0,3,2,1:T(8,128)} fusion(f32[128,4,8,128]{0,3,2,1:T(8,128)} %get-tuple-element.311, f32[4,512,128,8]{2,1,3,0:T(8,128)} %get-tuple-element.294, f32[4,8,128]{2,1,0:T(8,128)S(1)} %get-tuple-element.321, pred[128,512]{0,1:T(8,128)(4,1)S(1)} %broadcast_compare_fusion.2, f32[128,4,8]{0,2,1:T(8,128)S(1)} %get-tuple-element.295, ...), kind=kOutput, calls=%fused_computation.10.clone.1 | convolution fusion | flops 546832384 | bytes 13205509 | tf_op jit(solution)/shard_map/cond/branch_1_fun/while/body/eval_jaxpr/kgqn,nkd->qkgd/dot_general | solution.py:68
  144.7 1.8 fusion.89
  146.5 1.3 fusion.90
  147.8 0.1 broadcast_compare_fusion.2
  148.0 5.7 %fusion.87 = (f32[4,8,128]{2,1,0:T(8,128)S(1)}, f32[4,512,128,8]{2,1,3,0:T(8,128)}) fusion(pred[128,512]{0,1:T(8,128)(4,1)S(1)} %broadcast_compare_fusion.2, bf16[128,4,8,128]{3,0,2,1:T(8,128)(2,1)S(1)} %get-tuple-element.326, bf16[2048,4,128]{0,2,1:T(8,128)(2,1)} %get-tuple-element.325, s32[]{:T(128)S(6)} %select_n.46), kind=kOutput, calls=%fused_computation.4.clone.1 | convolution fusion | flops 543158272 | bytes 10043396 | tf_op jit(solution)/shard_map/cond/branch_1_fun/while/body/eval_jaxpr/qkgd,nkd->kgqn/dot_general | solution.py:60
  153.7 8.2 %bitcast_add_fusion.2 = f32[128,4,8,128]{0,3,2,1:T(8,128)} fusion(f32[128,4,8,128]{0,3,2,1:T(8,128)} %get-tuple-element.311, f32[4,512,128,8]{2,1,3,0:T(8,128)} %get-tuple-element.294, f32[4,8,128]{2,1,0:T(8,128)S(1)} %get-tuple-element.321, pred[128,512]{0,1:T(8,128)(4,1)S(1)} %broadcast_compare_fusion.2, f32[128,4,8]{0,2,1:T(8,128)S(1)} %get-tuple-element.295, ...), kind=kOutput, calls=%fused_computation.10.clone.1 | convolution fusion | flops 546832384 | bytes 13205509 | tf_op jit(solution)/shard_map/cond/branch_1_fun/while/body/eval_jaxpr/kgqn,nkd->qkgd/dot_general | solution.py:68
  161.9 1.8 fusion.89
  163.7 1.3 fusion.90
  165.1 1.8 divide_convert_fusion
  166.9 1.0 copy.28
  167.9 0.5 fusion.24
  168.4 0.5 fusion.26
  169.0 0.7 multiply_convert_fusion.1
  169.6 1.6 all-gather.8.cloned.1.call-done
  171.2 7.8 %and_dynamic-update-slice_fusion.7 = s32[4096,4096]{1,0:T(8,128)} fusion(s32[4096,512]{1,0:T(8,128)} %all-gather.8.cloned.1.call-done), kind=kLoop, calls=%fused_computation.37 | loop fusion | flops 4194303 | bytes 16777216
  179.0 4.3 %and_dynamic-update-slice_fusion.6 = s32[4096,4096]{1,0:T(8,128)} fusion(s32[4096,4096]{1,0:T(8,128)} %and_dynamic-update-slice_fusion.7, s32[4096,512]{1,0:T(8,128)S(1)} %copy-done.2), kind=kLoop, calls=%fused_computation.36 | loop fusion | flops 4194304 | bytes 16777216
  183.3 4.3 %and_dynamic-update-slice_fusion.5 = s32[4096,4096]{1,0:T(8,128)} fusion(s32[4096,4096]{1,0:T(8,128)} %and_dynamic-update-slice_fusion.6, s32[4096,512]{1,0:T(8,128)S(1)} %copy-done.2), kind=kLoop, calls=%fused_computation.35 | loop fusion | flops 4194304 | bytes 16777216
  187.5 4.2 %and_dynamic-update-slice_fusion.4 = s32[4096,4096]{1,0:T(8,128)} fusion(s32[4096,4096]{1,0:T(8,128)} %and_dynamic-update-slice_fusion.5, s32[4096,512]{1,0:T(8,128)S(1)} %copy-done.2), kind=kLoop, calls=%fused_computation.34 | loop fusion | flops 4194304 | bytes 16777216
  191.8 4.3 %and_dynamic-update-slice_fusion.3 = s32[4096,4096]{1,0:T(8,128)} fusion(s32[4096,4096]{1,0:T(8,128)} %and_dynamic-update-slice_fusion.4, s32[4096,512]{1,0:T(8,128)S(1)} %copy-done.2), kind=kLoop, calls=%fused_computation.33 | loop fusion | flops 4194304 | bytes 16777216
  196.0 4.2 %and_dynamic-update-slice_fusion.2 = s32[4096,4096]{1,0:T(8,128)} fusion(s32[4096,4096]{1,0:T(8,128)} %and_dynamic-update-slice_fusion.3, s32[4096,512]{1,0:T(8,128)S(1)} %copy-done.2), kind=kLoop, calls=%fused_computation.32 | loop fusion | flops 4194304 | bytes 16777216
  200.3 4.3 %and_dynamic-update-slice_fusion.1 = s32[4096,4096]{1,0:T(8,128)} fusion(s32[4096,4096]{1,0:T(8,128)} %and_dynamic-update-slice_fusion.2, s32[4096,512]{1,0:T(8,128)S(1)} %copy-done.2), kind=kLoop, calls=%fused_computation.31 | loop fusion | flops 4194304 | bytes 16777216
  204.6 4.3 %and_dynamic-update-slice_fusion = s32[4096,4096]{1,0:T(8,128)} fusion(s32[4096,4096]{1,0:T(8,128)} %and_dynamic-update-slice_fusion.1, s32[4096,512]{1,0:T(8,128)S(1)} %copy-done.2), kind=kLoop, calls=%fused_computation.30 | loop fusion | flops 4194304 | bytes 16777216 | tf_op jit(solution)/shard_map/concatenate | solution.py:54
  208.9 25.0 %fusion.23 = bf16[128,4096]{1,0:T(8,128)(2,1)} fusion(bf16[128,4096]{0,1:T(8,128)(2,1)S(1)} %bitcast.70, s32[4096,4096]{1,0:T(8,128)} %and_dynamic-update-slice_fusion, bf16[32,4096]{1,0:T(8,128)(2,1)S(1)} %copy-done, s32[4096]{0:T(1024)S(1)} %add_select_fusion), kind=kOutput, calls=%fused_computation.38 | convolution fusion | flops 5436473344 | bytes 69484544 | tf_op jit(solution)/shard_map/dot_general | solution.py:123
  (32 shorter events, 0.1 us)
Async XLA Ops:
  6.5 202.4 %copy-start = (bf16[32,4096]{1,0:T(8,128)(2,1)S(1)}, bf16[32,4096]{1,0:T(8,128)(2,1)}, u32[]{:S(2)}) copy-start(bf16[32,4096]{1,0:T(8,128)(2,1)} %param.14) | copy-start | bytes 786436
  6.5 46.7 %all-gather.4.cloned.1.call-start = ((), (), s32[]{:S(2)}) async-start(), calls=%async_computation | async-start | bytes 2228224 | tf_op jit(solution)/shard_map/all_gather | solution.py:94
  8.3 87.3 %all-gather.6.cloned.1.call-start = ((), (), s32[]{:S(2)}) async-start(), calls=%async_computation.1 | async-start | bytes 2228224 | tf_op jit(solution)/shard_map/all_gather | solution.py:95
  10.0 161.2 %all-gather.8.cloned.1.call-start = ((), (), s32[]{:S(2)}) async-start(), calls=%async_computation.2 | async-start | bytes 8912896 | tf_op jit(solution)/shard_map/all_gather | solution.py:122
  103.8 7.6 %copy-start.1 = (f32[4,512,128,8]{2,1,3,0:T(8,128)S(1)}, f32[4,512,128,8]{2,1,3,0:T(8,128)}, u32[]{:S(2)}) copy-start(f32[4,512,128,8]{2,1,3,0:T(8,128)} %get-tuple-element.294) | copy-start | bytes 25165828 | tf_op jit(solution)/shard_map/cond/branch_1_fun/while
  119.7 7.9 %copy-start.1 = (f32[4,512,128,8]{2,1,3,0:T(8,128)S(1)}, f32[4,512,128,8]{2,1,3,0:T(8,128)}, u32[]{:S(2)}) copy-start(f32[4,512,128,8]{2,1,3,0:T(8,128)} %get-tuple-element.294) | copy-start | bytes 25165828 | tf_op jit(solution)/shard_map/cond/branch_1_fun/while
  136.7 8.0 %copy-start.1 = (f32[4,512,128,8]{2,1,3,0:T(8,128)S(1)}, f32[4,512,128,8]{2,1,3,0:T(8,128)}, u32[]{:S(2)}) copy-start(f32[4,512,128,8]{2,1,3,0:T(8,128)} %get-tuple-element.294) | copy-start | bytes 25165828 | tf_op jit(solution)/shard_map/cond/branch_1_fun/while
  153.7 8.2 %copy-start.1 = (f32[4,512,128,8]{2,1,3,0:T(8,128)S(1)}, f32[4,512,128,8]{2,1,3,0:T(8,128)}, u32[]{:S(2)}) copy-start(f32[4,512,128,8]{2,1,3,0:T(8,128)} %get-tuple-element.294) | copy-start | bytes 25165828 | tf_op jit(solution)/shard_map/cond/branch_1_fun/while
  171.2 7.8 %copy-start.2 = (s32[4096,512]{1,0:T(8,128)S(1)}, s32[4096,512]{1,0:T(8,128)}, u32[]{:S(2)}) copy-start(s32[4096,512]{1,0:T(8,128)} %all-gather.8.cloned.1.call-done) | copy-start | bytes 25165828
Sparse Core Ops, SparseCore 0:
  9.5 43.7 all-gather.3
  55.4 40.1 all-gather.5
  97.8 73.3 all-gather.7
where the time goes:
time: 241 us; the launch traced here: 240 us
  waiting for transfers between devices  85.2 us (35%)
  matrix products  81.3 us (34%)
  other arithmetic  53.4 us (22%)
  between operations  13.7 us (6%)
  local copies, waits for them, and re-layouts  6.64 us (3%)
    all_gather x1, waiting for transfers between devices, local(): value_slice = lax.all_gather(values, 'blk', axis=0, tiled=True)  42.3 us
    all_gather x1, waiting for transfers between devices, local(): key_slice = lax.all_gather(keys, 'blk', axis=0, tiled=True)  40.6 us
    unnamed x7, other arithmetic  33.4 us
    dot_general x4, matrix products, update(): jnp.einsum('kgqn,nkd->qkgd', weights.astype(jnp.bfloat16), value_block, p...  31.6 us
    dot_general x1, matrix products, local(): mixed = jnp.dot(rotated, weight, preferred_element_type=jnp.float32)  25 us
    dot_general x4, matrix products, update(): jnp.einsum('qkgd,nkd->kgqn', query_tile, key_block, preferred_element_typ...  22.9 us
    reduce_sum x4, other arithmetic, update(): totals = totals * fading + jnp.sum(weights, axis=-1)  7.23 us
  transfers between devices with their start and end apart: 3, of which 3 were waited for; matrix products, arithmetic and copies ran while one was open for 32% of the time, Pallas kernels for 0%

commit v1 on v0

--- a/solution.py
+++ b/solution.py
@@ -92,7 +92,12 @@
     )
     last_position = jnp.max(query_positions)
     key_slice = lax.all_gather(keys, "blk", axis=0, tiled=True)
-    value_slice = lax.all_gather(values, "blk", axis=0, tiled=True)
+    ring = [values]
+    for hop in range(15):
+        ring.append(lax.ppermute(ring[-1], "blk", [(dev, (dev + 1) % 16) for dev in range(16)]))
+    value_slice = jnp.roll(
+        jnp.concatenate(ring[::-1], axis=0), (lax.axis_index("blk") + 1) * ring[0].shape[0], axis=0
+    )
     block_count = key_slice.shape[0]
     width = math.gcd(block_count, 512)
     heads_of_keys = key_slice.reshape(block_count, KEY_VALUE_HEADS, HEAD_SIZE)

time: 241 us -> 304 us (1.26)
  waiting for transfers between devices: 85.2 us -> 123 us
  local copies, waits for them, and re-layouts: 6.64 us -> 31.1 us
    ppermute x0 -> x15, waiting for transfers between devices: none -> 123 us  [local(): lax.ppermute(ring[-1], 'blk', [(dev, (dev + 1) % 16) for dev in range(16)])]
    all_gather x1 -> x0, waiting for transfers between devices: 42.3 us -> none  [local(): value_slice = lax.all_gather(values, 'blk', axis=0, tiled=True)]
    all_gather x1, waiting for transfers between devices: 40.6 us -> 0.01 us  [local(): key_slice = lax.all_gather(keys, 'blk', axis=0, tiled=True)]
    unnamed x6 -> x39, local copies, waits for them, and re-layouts: 3.37 us -> 23.9 us
    dynamic_slice x0 -> x1, local copies, waits for them, and re-layouts: none -> 4.21 us  [local(): jnp.roll(jnp.concatenate(ring[::-1], axis=0), (lax.axis_index('blk') + 1)...]
  transfers between devices with their start and end apart: 3 -> 17, of which waited for: 3 -> 15; matrix products, arithmetic and copies ran while one was open for 32% -> 33% of each run, Pallas kernels for 0% -> 0%
where the time goes in v1:
time: 304 us; the launch traced here: 303 us
  waiting for transfers between devices  123 us (40%)
  matrix products  80.4 us (26%)
  other arithmetic  53.5 us (18%)
  local copies, waits for them, and re-layouts  31.1 us (10%)
  between operations  14.1 us (5%)
    ppermute x15, waiting for transfers between devices, local(): lax.ppermute(ring[-1], 'blk', [(dev, (dev + 1) % 16) for dev in range(16)])  123 us
    unnamed x7, other arithmetic  33.5 us
    dot_general x4, matrix products, update(): jnp.einsum('kgqn,nkd->qkgd', weights.astype(jnp.bfloat16), value_block, p...  30.8 us
    dot_general x1, matrix products, local(): mixed = jnp.dot(rotated, weight, preferred_element_type=jnp.float32)  25 us
    unnamed x39, local copies, waits for them, and re-layouts  23.9 us
    dot_general x4, matrix products, update(): jnp.einsum('qkgd,nkd->kgqn', query_tile, key_block, preferred_element_typ...  23 us
    reduce_sum x4, other arithmetic, update(): totals = totals * fading + jnp.sum(weights, axis=-1)  7.23 us
  transfers between devices with their start and end apart: 17, of which 15 were waited for; matrix products, arithmetic and copies ran while one was open for 33% of the time, Pallas kernels for 0%

profile of v1, /device:TPU:0, one launch (start us, length us, event | category | flops | bytes accessed | tf_op | source)
XLA Modules:
  0.0 303.1 jit_solution(11428240326621935838)
XLA Ops:
  6.5 1.7 copy.30
  9.0 1.0 copy.31
  10.6 7.6 %collective-permute-done = bf16[128,512]{0,1:T(8,128)(2,1)S(1)} collective-permute-done((bf16[128,512]{0,1:T(8,128)(2,1)S(1)}, bf16[128,512]{0,1:T(8,128)(2,1)S(1)}, u32[]{:S(2)}, u32[]{:S(2)}) %collective-permute-start) | collective-permute-done | bytes 131104 | tf_op jit(solution)/shard_map/ppermute | solution.py:97
  18.2 7.2 %collective-permute-done.1 = bf16[128,512]{0,1:T(8,128)(2,1)S(1)} collective-permute-done((bf16[128,512]{0,1:T(8,128)(2,1)S(1)}, bf16[128,512]{0,1:T(8,128)(2,1)S(1)}, u32[]{:S(2)}, u32[]{:S(2)}) %collective-permute-start.1) | collective-permute-done | bytes 131104 | tf_op jit(solution)/shard_map/ppermute | solution.py:97
  25.5 7.7 %collective-permute-done.2 = bf16[128,512]{0,1:T(8,128)(2,1)S(1)} collective-permute-done((bf16[128,512]{0,1:T(8,128)(2,1)S(1)}, bf16[128,512]{0,1:T(8,128)(2,1)S(1)}, u32[]{:S(2)}, u32[]{:S(2)}) %collective-permute-start.2) | collective-permute-done | bytes 131104 | tf_op jit(solution)/shard_map/ppermute | solution.py:97
  33.2 7.1 %collective-permute-done.3 = bf16[128,512]{0,1:T(8,128)(2,1)S(1)} collective-permute-done((bf16[128,512]{0,1:T(8,128)(2,1)S(1)}, bf16[128,512]{0,1:T(8,128)(2,1)S(1)}, u32[]{:S(2)}, u32[]{:S(2)}) %collective-permute-start.3) | collective-permute-done | bytes 131104 | tf_op jit(solution)/shard_map/ppermute | solution.py:97
  40.2 9.3 %collective-permute-done.4 = bf16[128,512]{0,1:T(8,128)(2,1)S(1)} collective-permute-done((bf16[128,512]{0,1:T(8,128)(2,1)S(1)}, bf16[128,512]{0,1:T(8,128)(2,1)S(1)}, u32[]{:S(2)}, u32[]{:S(2)}) %collective-permute-start.4) | collective-permute-done | bytes 131104 | tf_op jit(solution)/shard_map/ppermute | solution.py:97
  49.6 7.1 %collective-permute-done.5 = bf16[128,512]{0,1:T(8,128)(2,1)S(1)} collective-permute-done((bf16[128,512]{0,1:T(8,128)(2,1)S(1)}, bf16[128,512]{0,1:T(8,128)(2,1)S(1)}, u32[]{:S(2)}, u32[]{:S(2)}) %collective-permute-start.5) | collective-permute-done | bytes 131104 | tf_op jit(solution)/shard_map/ppermute | solution.py:97
  56.6 7.1 %collective-permute-done.6 = bf16[128,512]{0,1:T(8,128)(2,1)S(1)} collective-permute-done((bf16[128,512]{0,1:T(8,128)(2,1)S(1)}, bf16[128,512]{0,1:T(8,128)(2,1)S(1)}, u32[]{:S(2)}, u32[]{:S(2)}) %collective-permute-start.6) | collective-permute-done | bytes 131104 | tf_op jit(solution)/shard_map/ppermute | solution.py:97
  63.7 7.3 %collective-permute-done.7 = bf16[128,512]{0,1:T(8,128)(2,1)S(1)} collective-permute-done((bf16[128,512]{0,1:T(8,128)(2,1)S(1)}, bf16[128,512]{0,1:T(8,128)(2,1)S(1)}, u32[]{:S(2)}, u32[]{:S(2)}) %collective-permute-start.7) | collective-permute-done | bytes 131104 | tf_op jit(solution)/shard_map/ppermute | solution.py:97
  71.0 10.0 %collective-permute-done.8 = bf16[128,512]{0,1:T(8,128)(2,1)S(1)} collective-permute-done((bf16[128,512]{0,1:T(8,128)(2,1)S(1)}, bf16[128,512]{0,1:T(8,128)(2,1)S(1)}, u32[]{:S(2)}, u32[]{:S(2)}) %collective-permute-start.8) | collective-permute-done | bytes 131104 | tf_op jit(solution)/shard_map/ppermute | solution.py:97
  81.0 9.4 %collective-permute-done.9 = bf16[128,512]{0,1:T(8,128)(2,1)S(1)} collective-permute-done((bf16[128,512]{0,1:T(8,128)(2,1)S(1)}, bf16[128,512]{0,1:T(8,128)(2,1)S(1)}, u32[]{:S(2)}, u32[]{:S(2)}) %collective-permute-start.9) | collective-permute-done | bytes 131104 | tf_op jit(solution)/shard_map/ppermute | solution.py:97
  90.5 7.2 %collective-permute-done.10 = bf16[128,512]{0,1:T(8,128)(2,1)S(1)} collective-permute-done((bf16[128,512]{0,1:T(8,128)(2,1)S(1)}, bf16[128,512]{0,1:T(8,128)(2,1)S(1)}, u32[]{:S(2)}, u32[]{:S(2)}) %collective-permute-start.10) | collective-permute-done | bytes 131104 | tf_op jit(solution)/shard_map/ppermute | solution.py:97
  97.7 10.0 %collective-permute-done.11 = bf16[128,512]{0,1:T(8,128)(2,1)S(1)} collective-permute-done((bf16[128,512]{0,1:T(8,128)(2,1)S(1)}, bf16[128,512]{0,1:T(8,128)(2,1)S(1)}, u32[]{:S(2)}, u32[]{:S(2)}) %collective-permute-start.11) | collective-permute-done | bytes 131104 | tf_op jit(solution)/shard_map/ppermute | solution.py:97
  107.7 10.0 %collective-permute-done.12 = bf16[128,512]{0,1:T(8,128)(2,1)S(1)} collective-permute-done((bf16[128,512]{0,1:T(8,128)(2,1)S(1)}, bf16[128,512]{0,1:T(8,128)(2,1)S(1)}, u32[]{:S(2)}, u32[]{:S(2)}) %collective-permute-start.12) | collective-permute-done | bytes 131104 | tf_op jit(solution)/shard_map/ppermute | solution.py:97
  117.8 0.7 fusion.47
  118.5 6.6 %collective-permute-done.13 = bf16[128,512]{0,1:T(8,128)(2,1)S(1)} collective-permute-done((bf16[128,512]{0,1:T(8,128)(2,1)S(1)}, bf16[128,512]{0,1:T(8,128)(2,1)S(1)}, u32[]{:S(2)}, u32[]{:S(2)}) %collective-permute-start.13) | collective-permute-done | bytes 131104 | tf_op jit(solution)/shard_map/ppermute | solution.py:97
  126.3 8.8 %collective-permute-done.14 = bf16[128,512]{0,1:T(8,128)(2,1)S(1)} collective-permute-done((bf16[128,512]{0,1:T(8,128)(2,1)S(1)}, bf16[128,512]{0,1:T(8,128)(2,1)S(1)}, u32[]{:S(2)}, u32[]{:S(2)}) %collective-permute-start.14) | collective-permute-done | bytes 131104 | tf_op jit(solution)/shard_map/ppermute | solution.py:97
  152.8 0.7 constant_dynamic-update-slice_fusion.5
  156.9 71.9 %conditional.1 = (f32[4,8,128]{2,1,0:T(8,128)}, f32[128,4,8,128]{0,3,2,1:T(8,128)}) conditional(s32[]{:T(128)} %convert_element_type.53, () %tuple.41, (bf16[2048,512]{0,1:T(8,128)(2,1)}, s32[]{:T(128)}, s32[]{:T(128)}, bf16[4096,512]{0,1:T(8,128)(2,1)}, bf16[128,4096]{1,0:T(8,128)(2,1)S(1)}, /*index=5*/s32[128]{0:T(128)S(1)}, s32[]{:T(128)}, ...), branch_computations={%region_1.2_spmd, %region_2.7_spmd.clone} | conditional | flops 1098473984 | bytes 73929704 | solution.py:119
  156.9 4.2 %constant_dynamic-slice_fusion = bf16[2048,512]{0,1:T(8,128)(2,1)} fusion(bf16[4096,512]{0,1:T(8,128)(2,1)} %get-tuple-element.261, s32[]{:T(128)S(6)} %select_n.47), kind=kLoop, calls=%fused_computation.28 | loop fusion | bytes 4194308 | tf_op jit(solution)/shard_map/jit(_roll_dynamic)/dynamic_slice | solution.py:98
  162.5 66.4 %while.27 = (s32[]{:T(128)}, f32[4,8,128]{2,1,0:T(8,128)S(1)}, f32[4,8,128]{2,1,0:T(8,128)}, f32[128,4,8,128]{0,3,2,1:T(8,128)}, s32[128]{0:T(128)S(1)}, /*index...) while((s32[]{:T(128)}, f32[4,8,128]{2,1,0:T(8,128)S(1)}, ...), condition=%wide.region_6.6_spmd.clone, body=%wide.region_3.5_spmd.clone.sunk | while | flops 1098473984 | bytes 65540820 | solution.py:117
  162.7 5.7 %fusion.87 = (f32[4,8,128]{2,1,0:T(8,128)S(1)}, f32[4,512,128,8]{2,1,3,0:T(8,128)}) fusion(pred[128,512]{0,1:T(8,128)(4,1)S(1)} %broadcast_compare_fusion.2, bf16[128,4,8,128]{3,0,2,1:T(8,128)(2,1)S(1)} %get-tuple-element.447, bf16[2048,4,128]{0,2,1:T(8,128)(2,1)} %get-tuple-element.446, s32[]{:T(128)S(6)} %select_n.68), kind=kOutput, calls=%fused_computation.4.clone.1 | convolution fusion | flops 543158272 | bytes 10043396 | tf_op jit(solution)/shard_map/cond/branch_1_fun/while/body/eval_jaxpr/qkgd,nkd->kgqn/dot_general | solution.py:60
  168.4 7.2 %bitcast_add_fusion.2 = f32[128,4,8,128]{0,3,2,1:T(8,128)} fusion(f32[128,4,8,128]{0,3,2,1:T(8,128)} %get-tuple-element.432, f32[4,512,128,8]{2,1,3,0:T(8,128)} %get-tuple-element.415, f32[4,8,128]{2,1,0:T(8,128)S(1)} %get-tuple-element.442, pred[128,512]{0,1:T(8,128)(4,1)S(1)} %broadcast_compare_fusion.2, f32[128,4,8]{0,2,1:T(8,128)S(1)} %get-tuple-element.416, ...), kind=kOutput, calls=%fused_computation.10.clone.1 | convolution fusion | flops 546832384 | bytes 13205509 | tf_op jit(solution)/shard_map/cond/branch_1_fun/while/body/eval_jaxpr/kgqn,nkd->qkgd/dot_general | solution.py:68
  175.7 1.8 fusion.89
  178.3 5.7 %fusion.87 = (f32[4,8,128]{2,1,0:T(8,128)S(1)}, f32[4,512,128,8]{2,1,3,0:T(8,128)}) fusion(pred[128,512]{0,1:T(8,128)(4,1)S(1)} %broadcast_compare_fusion.2, bf16[128,4,8,128]{3,0,2,1:T(8,128)(2,1)S(1)} %get-tuple-element.447, bf16[2048,4,128]{0,2,1:T(8,128)(2,1)} %get-tuple-element.446, s32[]{:T(128)S(6)} %select_n.68), kind=kOutput, calls=%fused_computation.4.clone.1 | convolution fusion | flops 543158272 | bytes 10043396 | tf_op jit(solution)/shard_map/cond/branch_1_fun/while/body/eval_jaxpr/qkgd,nkd->kgqn/dot_general | solution.py:60
  184.1 7.8 %bitcast_add_fusion.2 = f32[128,4,8,128]{0,3,2,1:T(8,128)} fusion(f32[128,4,8,128]{0,3,2,1:T(8,128)} %get-tuple-element.432, f32[4,512,128,8]{2,1,3,0:T(8,128)} %get-tuple-element.415, f32[4,8,128]{2,1,0:T(8,128)S(1)} %get-tuple-element.442, pred[128,512]{0,1:T(8,128)(4,1)S(1)} %broadcast_compare_fusion.2, f32[128,4,8]{0,2,1:T(8,128)S(1)} %get-tuple-element.416, ...), kind=kOutput, calls=%fused_computation.10.clone.1 | convolution fusion | flops 546832384 | bytes 13205509 | tf_op jit(solution)/shard_map/cond/branch_1_fun/while/body/eval_jaxpr/kgqn,nkd->qkgd/dot_general | solution.py:68
  191.9 1.8 fusion.89
  193.7 1.3 fusion.90
  195.2 5.7 %fusion.87 = (f32[4,8,128]{2,1,0:T(8,128)S(1)}, f32[4,512,128,8]{2,1,3,0:T(8,128)}) fusion(pred[128,512]{0,1:T(8,128)(4,1)S(1)} %broadcast_compare_fusion.2, bf16[128,4,8,128]{3,0,2,1:T(8,128)(2,1)S(1)} %get-tuple-element.447, bf16[2048,4,128]{0,2,1:T(8,128)(2,1)} %get-tuple-element.446, s32[]{:T(128)S(6)} %select_n.68), kind=kOutput, calls=%fused_computation.4.clone.1 | convolution fusion | flops 543158272 | bytes 10043396 | tf_op jit(solution)/shard_map/cond/branch_1_fun/while/body/eval_jaxpr/qkgd,nkd->kgqn/dot_general | solution.py:60
  201.0 7.8 %bitcast_add_fusion.2 = f32[128,4,8,128]{0,3,2,1:T(8,128)} fusion(f32[128,4,8,128]{0,3,2,1:T(8,128)} %get-tuple-element.432, f32[4,512,128,8]{2,1,3,0:T(8,128)} %get-tuple-element.415, f32[4,8,128]{2,1,0:T(8,128)S(1)} %get-tuple-element.442, pred[128,512]{0,1:T(8,128)(4,1)S(1)} %broadcast_compare_fusion.2, f32[128,4,8]{0,2,1:T(8,128)S(1)} %get-tuple-element.416, ...), kind=kOutput, calls=%fused_computation.10.clone.1 | convolution fusion | flops 546832384 | bytes 13205509 | tf_op jit(solution)/shard_map/cond/branch_1_fun/while/body/eval_jaxpr/kgqn,nkd->qkgd/dot_general | solution.py:68
  208.8 1.8 fusion.89
  210.6 1.3 fusion.90
  212.1 5.7 %fusion.87 = (f32[4,8,128]{2,1,0:T(8,128)S(1)}, f32[4,512,128,8]{2,1,3,0:T(8,128)}) fusion(pred[128,512]{0,1:T(8,128)(4,1)S(1)} %broadcast_compare_fusion.2, bf16[128,4,8,128]{3,0,2,1:T(8,128)(2,1)S(1)} %get-tuple-element.447, bf16[2048,4,128]{0,2,1:T(8,128)(2,1)} %get-tuple-element.446, s32[]{:T(128)S(6)} %select_n.68), kind=kOutput, calls=%fused_computation.4.clone.1 | convolution fusion | flops 543158272 | bytes 10043396 | tf_op jit(solution)/shard_map/cond/branch_1_fun/while/body/eval_jaxpr/qkgd,nkd->kgqn/dot_general | solution.py:60
  217.9 7.8 %bitcast_add_fusion.2 = f32[128,4,8,128]{0,3,2,1:T(8,128)} fusion(f32[128,4,8,128]{0,3,2,1:T(8,128)} %get-tuple-element.432, f32[4,512,128,8]{2,1,3,0:T(8,128)} %get-tuple-element.415, f32[4,8,128]{2,1,0:T(8,128)S(1)} %get-tuple-element.442, pred[128,512]{0,1:T(8,128)(4,1)S(1)} %broadcast_compare_fusion.2, f32[128,4,8]{0,2,1:T(8,128)S(1)} %get-tuple-element.416, ...), kind=kOutput, calls=%fused_computation.10.clone.1 | convolution fusion | flops 546832384 | bytes 13205509 | tf_op jit(solution)/shard_map/cond/branch_1_fun/while/body/eval_jaxpr/kgqn,nkd->qkgd/dot_general | solution.py:68
  225.7 1.8 fusion.89
  227.5 1.3 fusion.90
  228.9 1.9 divide_convert_fusion
  230.7 1.0 copy.35
  233.5 7.8 %and_dynamic-update-slice_fusion.7 = s32[4096,4096]{1,0:T(8,128)} fusion(s32[4096,512]{1,0:T(8,128)} %all-gather.5.cloned.1.call-done), kind=kLoop, calls=%fused_computation.38 | loop fusion | flops 4194303 | bytes 16777216
  241.3 4.3 %and_dynamic-update-slice_fusion.6 = s32[4096,4096]{1,0:T(8,128)} fusion(s32[4096,4096]{1,0:T(8,128)} %and_dynamic-update-slice_fusion.7, s32[4096,512]{1,0:T(8,128)S(1)} %copy-done.2), kind=kLoop, calls=%fused_computation.37 | loop fusion | flops 4194304 | bytes 16777216
  245.6 4.4 %and_dynamic-update-slice_fusion.5 = s32[4096,4096]{1,0:T(8,128)} fusion(s32[4096,4096]{1,0:T(8,128)} %and_dynamic-update-slice_fusion.6, s32[4096,512]{1,0:T(8,128)S(1)} %copy-done.2), kind=kLoop, calls=%fused_computation.36 | loop fusion | flops 4194304 | bytes 16777216
  250.0 4.3 %and_dynamic-update-slice_fusion.4 = s32[4096,4096]{1,0:T(8,128)} fusion(s32[4096,4096]{1,0:T(8,128)} %and_dynamic-update-slice_fusion.5, s32[4096,512]{1,0:T(8,128)S(1)} %copy-done.2), kind=kLoop, calls=%fused_computation.35 | loop fusion | flops 4194304 | bytes 16777216
  254.2 4.3 %and_dynamic-update-slice_fusion.3 = s32[4096,4096]{1,0:T(8,128)} fusion(s32[4096,4096]{1,0:T(8,128)} %and_dynamic-update-slice_fusion.4, s32[4096,512]{1,0:T(8,128)S(1)} %copy-done.2), kind=kLoop, calls=%fused_computation.34 | loop fusion | flops 4194304 | bytes 16777216
  258.5 4.3 %and_dynamic-update-slice_fusion.2 = s32[4096,4096]{1,0:T(8,128)} fusion(s32[4096,4096]{1,0:T(8,128)} %and_dynamic-update-slice_fusion.3, s32[4096,512]{1,0:T(8,128)S(1)} %copy-done.2), kind=kLoop, calls=%fused_computation.33 | loop fusion | flops 4194304 | bytes 16777216
  262.7 4.2 %and_dynamic-update-slice_fusion.1 = s32[4096,4096]{1,0:T(8,128)} fusion(s32[4096,4096]{1,0:T(8,128)} %and_dynamic-update-slice_fusion.2, s32[4096,512]{1,0:T(8,128)S(1)} %copy-done.2), kind=kLoop, calls=%fused_computation.32 | loop fusion | flops 4194304 | bytes 16777216
  267.0 4.2 %and_dynamic-update-slice_fusion = s32[4096,4096]{1,0:T(8,128)} fusion(s32[4096,4096]{1,0:T(8,128)} %and_dynamic-update-slice_fusion.1, s32[4096,512]{1,0:T(8,128)S(1)} %copy-done.2), kind=kLoop, calls=%fused_computation.31 | loop fusion | flops 4194304 | bytes 16777216 | tf_op jit(solution)/shard_map/concatenate | solution.py:54
  271.2 25.0 %fusion.23 = bf16[128,4096]{1,0:T(8,128)(2,1)} fusion(bf16[128,4096]{0,1:T(8,128)(2,1)S(1)} %bitcast.70, s32[4096,4096]{1,0:T(8,128)} %and_dynamic-update-slice_fusion, bf16[32,4096]{1,0:T(8,128)(2,1)S(1)} %copy-done, s32[4096]{0:T(1024)S(1)} %add_select_fusion), kind=kOutput, calls=%fused_computation.39 | convolution fusion | flops 5436473344 | bytes 69484544 | tf_op jit(solution)/shard_map/dot_general | solution.py:128
  (94 shorter events, 27.4 us)
Async XLA Ops:
  6.5 264.7 %copy-start = (bf16[32,4096]{1,0:T(8,128)(2,1)S(1)}, bf16[32,4096]{1,0:T(8,128)(2,1)}, u32[]{:S(2)}) copy-start(bf16[32,4096]{1,0:T(8,128)(2,1)} %param.14) | copy-start | bytes 786436
  6.5 150.4 %all-gather.3.cloned.1.call-start = ((), (), s32[]{:S(2)}) async-start(), calls=%async_computation | async-start | bytes 2228224 | tf_op jit(solution)/shard_map/all_gather | solution.py:94
  8.3 225.2 %all-gather.5.cloned.1.call-start = ((), (), s32[]{:S(2)}) async-start(), calls=%async_computation.1 | async-start | bytes 8912896 | tf_op jit(solution)/shard_map/all_gather | solution.py:127
  10.1 8.2 %collective-permute-start = (bf16[128,512]{0,1:T(8,128)(2,1)S(1)}, bf16[128,512]{0,1:T(8,128)(2,1)S(1)}, u32[]{:S(2)}, u32[]{:S(2)}) collective-permute-start(bf16[128,512]{0,1:T(8,128)(2,1)S(1)} %copy.31), channel_id=1, source_target_pairs={{0,1},{1,2},{2,3},{3,4},{4,5},{5,6},{6,7},{7,8},{8,9},{9,10},{10,1... | collective-permute-start | bytes 393224 | tf_op jit(solution)/shard_map/ppermute | solution.py:97
  18.2 7.3 %collective-permute-start.1 = (bf16[128,512]{0,1:T(8,128)(2,1)S(1)}, bf16[128,512]{0,1:T(8,128)(2,1)S(1)}, u32[]{:S(2)}, u32[]{:S(2)}) collective-permute-start(bf16[128,512]{0,1:T(8,128)(2,1)S(1)} %collective-permute-done), channel_id=1, source_target_pairs={{0,1},{1,2},{2,3},{3,4},{4,5},{5,6},{6,7},{7,8},{8,9},{9,10},{10,1... | collective-permute-start | bytes 393224 | tf_op jit(solution)/shard_map/ppermute | solution.py:97
  25.5 7.7 %collective-permute-start.2 = (bf16[128,512]{0,1:T(8,128)(2,1)S(1)}, bf16[128,512]{0,1:T(8,128)(2,1)S(1)}, u32[]{:S(2)}, u32[]{:S(2)}) collective-permute-start(bf16[128,512]{0,1:T(8,128)(2,1)S(1)} %collective-permute-done.1), channel_id=1, source_target_pairs={{0,1},{1,2},{2,3},{3,4},{4,5},{5,6},{6,7},{7,8},{8,9},{9,10},{10,1... | collective-permute-start | bytes 393224 | tf_op jit(solution)/shard_map/ppermute | solution.py:97
  33.2 7.1 %collective-permute-start.3 = (bf16[128,512]{0,1:T(8,128)(2,1)S(1)}, bf16[128,512]{0,1:T(8,128)(2,1)S(1)}, u32[]{:S(2)}, u32[]{:S(2)}) collective-permute-start(bf16[128,512]{0,1:T(8,128)(2,1)S(1)} %collective-permute-done.2), channel_id=1, source_target_pairs={{0,1},{1,2},{2,3},{3,4},{4,5},{5,6},{6,7},{7,8},{8,9},{9,10},{10,1... | collective-permute-start | bytes 393224 | tf_op jit(solution)/shard_map/ppermute | solution.py:97
  40.2 9.3 %collective-permute-start.4 = (bf16[128,512]{0,1:T(8,128)(2,1)S(1)}, bf16[128,512]{0,1:T(8,128)(2,1)S(1)}, u32[]{:S(2)}, u32[]{:S(2)}) collective-permute-start(bf16[128,512]{0,1:T(8,128)(2,1)S(1)} %collective-permute-done.3), channel_id=1, source_target_pairs={{0,1},{1,2},{2,3},{3,4},{4,5},{5,6},{6,7},{7,8},{8,9},{9,10},{10,1... | collective-permute-start | bytes 393224 | tf_op jit(solution)/shard_map/ppermute | solution.py:97
  49.6 7.1 %collective-permute-start.5 = (bf16[128,512]{0,1:T(8,128)(2,1)S(1)}, bf16[128,512]{0,1:T(8,128)(2,1)S(1)}, u32[]{:S(2)}, u32[]{:S(2)}) collective-permute-start(bf16[128,512]{0,1:T(8,128)(2,1)S(1)} %collective-permute-done.4), channel_id=1, source_target_pairs={{0,1},{1,2},{2,3},{3,4},{4,5},{5,6},{6,7},{7,8},{8,9},{9,10},{10,1... | collective-permute-start | bytes 393224 | tf_op jit(solution)/shard_map/ppermute | solution.py:97
  56.6 7.1 %collective-permute-start.6 = (bf16[128,512]{0,1:T(8,128)(2,1)S(1)}, bf16[128,512]{0,1:T(8,128)(2,1)S(1)}, u32[]{:S(2)}, u32[]{:S(2)}) collective-permute-start(bf16[128,512]{0,1:T(8,128)(2,1)S(1)} %collective-permute-done.5), channel_id=1, source_target_pairs={{0,1},{1,2},{2,3},{3,4},{4,5},{5,6},{6,7},{7,8},{8,9},{9,10},{10,1... | collective-permute-start | bytes 393224 | tf_op jit(solution)/shard_map/ppermute | solution.py:97
  63.7 7.3 %collective-permute-start.7 = (bf16[128,512]{0,1:T(8,128)(2,1)S(1)}, bf16[128,512]{0,1:T(8,128)(2,1)S(1)}, u32[]{:S(2)}, u32[]{:S(2)}) collective-permute-start(bf16[128,512]{0,1:T(8,128)(2,1)S(1)} %collective-permute-done.6), channel_id=1, source_target_pairs={{0,1},{1,2},{2,3},{3,4},{4,5},{5,6},{6,7},{7,8},{8,9},{9,10},{10,1... | collective-permute-start | bytes 393224 | tf_op jit(solution)/shard_map/ppermute | solution.py:97
  71.0 10.0 %collective-permute-start.8 = (bf16[128,512]{0,1:T(8,128)(2,1)S(1)}, bf16[128,512]{0,1:T(8,128)(2,1)S(1)}, u32[]{:S(2)}, u32[]{:S(2)}) collective-permute-start(bf16[128,512]{0,1:T(8,128)(2,1)S(1)} %collective-permute-done.7), channel_id=1, source_target_pairs={{0,1},{1,2},{2,3},{3,4},{4,5},{5,6},{6,7},{7,8},{8,9},{9,10},{10,1... | collective-permute-start | bytes 393224 | tf_op jit(solution)/shard_map/ppermute | solution.py:97
  81.0 9.4 %collective-permute-start.9 = (bf16[128,512]{0,1:T(8,128)(2,1)S(1)}, bf16[128,512]{0,1:T(8,128)(2,1)S(1)}, u32[]{:S(2)}, u32[]{:S(2)}) collective-permute-start(bf16[128,512]{0,1:T(8,128)(2,1)S(1)} %collective-permute-done.8), channel_id=1, source_target_pairs={{0,1},{1,2},{2,3},{3,4},{4,5},{5,6},{6,7},{7,8},{8,9},{9,10},{10,1... | collective-permute-start | bytes 393224 | tf_op jit(solution)/shard_map/ppermute | solution.py:97
  90.5 7.2 %collective-permute-start.10 = (bf16[128,512]{0,1:T(8,128)(2,1)S(1)}, bf16[128,512]{0,1:T(8,128)(2,1)S(1)}, u32[]{:S(2)}, u32[]{:S(2)}) collective-permute-start(bf16[128,512]{0,1:T(8,128)(2,1)S(1)} %collective-permute-done.9), channel_id=1, source_target_pairs={{0,1},{1,2},{2,3},{3,4},{4,5},{5,6},{6,7},{7,8},{8,9},{9,10},{10,1... | collective-permute-start | bytes 393224 | tf_op jit(solution)/shard_map/ppermute | solution.py:97
  97.7 10.0 %collective-permute-start.11 = (bf16[128,512]{0,1:T(8,128)(2,1)S(1)}, bf16[128,512]{0,1:T(8,128)(2,1)S(1)}, u32[]{:S(2)}, u32[]{:S(2)}) collective-permute-start(bf16[128,512]{0,1:T(8,128)(2,1)S(1)} %collective-permute-done.10), channel_id=1, source_target_pairs={{0,1},{1,2},{2,3},{3,4},{4,5},{5,6},{6,7},{7,8},{8,9},{9,10},{10,1... | collective-permute-start | bytes 393224 | tf_op jit(solution)/shard_map/ppermute | solution.py:97
  107.7 10.0 %collective-permute-start.12 = (bf16[128,512]{0,1:T(8,128)(2,1)S(1)}, bf16[128,512]{0,1:T(8,128)(2,1)S(1)}, u32[]{:S(2)}, u32[]{:S(2)}) collective-permute-start(bf16[128,512]{0,1:T(8,128)(2,1)S(1)} %collective-permute-done.11), channel_id=1, source_target_pairs={{0,1},{1,2},{2,3},{3,4},{4,5},{5,6},{6,7},{7,8},{8,9},{9,10},{10,1... | collective-permute-start | bytes 393224 | tf_op jit(solution)/shard_map/ppermute | solution.py:97
  117.8 7.3 %collective-permute-start.13 = (bf16[128,512]{0,1:T(8,128)(2,1)S(1)}, bf16[128,512]{0,1:T(8,128)(2,1)S(1)}, u32[]{:S(2)}, u32[]{:S(2)}) collective-permute-start(bf16[128,512]{0,1:T(8,128)(2,1)S(1)} %collective-permute-done.12), channel_id=1, source_target_pairs={{0,1},{1,2},{2,3},{3,4},{4,5},{5,6},{6,7},{7,8},{8,9},{9,10},{10,1... | collective-permute-start | bytes 393224 | tf_op jit(solution)/shard_map/ppermute | solution.py:97
  125.1 10.1 %collective-permute-start.14 = (bf16[128,512]{0,1:T(8,128)(2,1)S(1)}, bf16[128,512]{0,1:T(8,128)(2,1)S(1)}, u32[]{:S(2)}, u32[]{:S(2)}) collective-permute-start(bf16[128,512]{0,1:T(8,128)(2,1)S(1)} %collective-permute-done.13), channel_id=1, source_target_pairs={{0,1},{1,2},{2,3},{3,4},{4,5},{5,6},{6,7},{7,8},{8,9},{9,10},{10,1... | collective-permute-start | bytes 393224 | tf_op jit(solution)/shard_map/ppermute | solution.py:97
  126.3 30.7 %copy-start.3 = (bf16[128,4096]{1,0:T(8,128)(2,1)S(1)}, bf16[128,4096]{1,0:T(8,128)(2,1)}, u32[]{:S(2)}) copy-start(bf16[128,4096]{1,0:T(8,128)(2,1)} %param.10) | copy-start | bytes 3145732
  168.4 7.3 %copy-start.1 = (f32[4,512,128,8]{2,1,3,0:T(8,128)S(1)}, f32[4,512,128,8]{2,1,3,0:T(8,128)}, u32[]{:S(2)}) copy-start(f32[4,512,128,8]{2,1,3,0:T(8,128)} %get-tuple-element.415) | copy-start | bytes 25165828 | tf_op jit(solution)/shard_map/cond/branch_1_fun/while
  184.0 7.8 %copy-start.1 = (f32[4,512,128,8]{2,1,3,0:T(8,128)S(1)}, f32[4,512,128,8]{2,1,3,0:T(8,128)}, u32[]{:S(2)}) copy-start(f32[4,512,128,8]{2,1,3,0:T(8,128)} %get-tuple-element.415) | copy-start | bytes 25165828 | tf_op jit(solution)/shard_map/cond/branch_1_fun/while
  201.0 7.9 %copy-start.1 = (f32[4,512,128,8]{2,1,3,0:T(8,128)S(1)}, f32[4,512,128,8]{2,1,3,0:T(8,128)}, u32[]{:S(2)}) copy-start(f32[4,512,128,8]{2,1,3,0:T(8,128)} %get-tuple-element.415) | copy-start | bytes 25165828 | tf_op jit(solution)/shard_map/cond/branch_1_fun/while
  217.9 7.8 %copy-start.1 = (f32[4,512,128,8]{2,1,3,0:T(8,128)S(1)}, f32[4,512,128,8]{2,1,3,0:T(8,128)}, u32[]{:S(2)}) copy-start(f32[4,512,128,8]{2,1,3,0:T(8,128)} %get-tuple-element.415) | copy-start | bytes 25165828 | tf_op jit(solution)/shard_map/cond/branch_1_fun/while
  233.4 7.8 %copy-start.2 = (s32[4096,512]{1,0:T(8,128)S(1)}, s32[4096,512]{1,0:T(8,128)}, u32[]{:S(2)}) copy-start(s32[4096,512]{1,0:T(8,128)} %all-gather.5.cloned.1.call-done) | copy-start | bytes 25165828
Sparse Core Ops, SparseCore 0:
  9.5 46.3 all-gather.2
  58.0 78.6 all-gather.4
